TPU v7x, 512 devices: a whole 4x8x8 slice. The times are simulated.
512 devices in a mesh: cols: 4 (over x), rows: 128 (over y, z, core).
Axes of the slice: x: 4, y: 8, z: 8, core: 2. Of those that a mesh axis runs over, the one named last changes fastest.
Arguments:
- gradient: float32 [128, 131072], P('cols', 'rows'), may hold values from -100 to 100
- width_factor: float32 [128, 128], P(None, 'cols'), may hold values from -3 to 4, as said below
- diag_blocks: float32 [1024, 128, 128], P('rows'), may hold values from -2 to 24, as said below
- jacobi_inverse: float32 [1024, 128, 128], P('rows'), may hold values from -2 to 2, as said below
- coupling_tiles: bfloat16 [8192, 128, 128], P('rows'), may hold values from -4 to 4, as said below
- tile_local: int32 [8192], P('rows'), may hold values from 0 to 7
- tile_remote: int32 [8192], P('rows'), may hold values from 0 to 1023, as said below
- tile_count: int32 [128], P('rows'), may hold values from 0 to 63, as said below
Outputs:
- solution: float32 [128, 131072], P('cols', 'rows')
- residual: float32 [128, 131072], P('cols', 'rows')
Inputs may be any that keep to these rules, and one draw needn't show every extreme that they name: `tile_remote`: the live entries are the first tile_count entries of each device's list; they name distinct devices other than the owner, each at most once. For a live entry of device d naming block J of device e, device e has a live entry naming d's block with its tile the transpose. Pad entries hold valid indices. `tile_count`: at most 63 on one device, reached on some device. `coupling_tiles`: with diag_blocks and the live entries, M is symmetric positive definite. `diag_blocks`: symmetric positive definite tiles. `jacobi_inverse`: the inverses of diag_blocks, symmetric. `width_factor`: symmetric positive definite.
All inputs are finite; a program needn't handle non-finite values.
Results may differ from a plain program's by a relative error of at most 0.0085.
Values may be sent and summed in bfloat16 or wider, within the bound.
A program may use at most 64 MiB of HBM per device.

v0:
```python
import functools

import jax
import jax.numpy as jnp
from jax import lax
from jax.sharding import Mesh
from jax.sharding import PartitionSpec as P

BLOCK = 128
ITERS = 6
ROWS = ("rows_0", "rows_1", "rows_2")
COLS_ROWS = ("cols", "rows_0", "rows_1", "rows_2")


highest = lax.Precision.HIGHEST


def in_blocks(array, dim, peers):
    dims = array.shape
    pieces = array.reshape(*dims[:dim], peers, dims[dim] // peers, *dims[dim + 1 :])
    return jnp.moveaxis(pieces, dim, 0)


def sum_at_owner(array, axis, dim):
    pieces = in_blocks(array, dim, lax.axis_size(axis))
    arrived = lax.all_to_all(pieces, axis, split_axis=0, concat_axis=0, tiled=True)
    return arrived.sum(axis=0)


def over_axes(array, axes):
    return functools.reduce(lax.psum, axes, array)


def on_device(
    gradient,
    width_factor,
    diag_blocks,
    jacobi_inverse,
    coupling_tiles,
    tile_local,
    tile_remote,
    tile_count,
):
    width_dev, rows_dev = gradient.shape
    blocks_dev = diag_blocks.shape[0]
    slot_count = tile_local.shape[0]
    devices = lax.axis_size(ROWS)
    active_slot = jnp.arange(slot_count, dtype=jnp.int32) < tile_count[0]
    placing = (
        (tile_local[:, None] == jnp.arange(blocks_dev, dtype=jnp.int32)[None, :])
        & active_slot[:, None]
    ).astype(jnp.float32)
    owner_dev = tile_remote // blocks_dev
    matches = active_slot[:, None] & (
        owner_dev[:, None] == jnp.arange(devices, dtype=jnp.int32)[None, :]
    )
    request = jnp.sum(jnp.where(matches, (tile_remote % blocks_dev)[:, None], 0), axis=0)
    granted = lax.all_to_all(request, ROWS, split_axis=0, concat_axis=0, tiled=True)

    def precondition(vector):
        blocks = vector.reshape(width_dev, blocks_dev, BLOCK)
        return jnp.einsum("enj,nji->eni", blocks, jacobi_inverse, precision=highest).reshape(
            width_dev, rows_dev
        )

    solution = jnp.zeros_like(gradient)
    residual = gradient
    precond_res = precondition(residual)
    direction = precond_res
    res_norm = over_axes(jnp.sum(residual * precond_res), COLS_ROWS)
    for iteration in range(ITERS):
        apply_blocks = direction.reshape(width_dev, blocks_dev, BLOCK)
        local_part = jnp.einsum("enj,nji->eni", apply_blocks, diag_blocks, precision=highest)
        rounded = direction.astype(jnp.bfloat16).reshape(width_dev, blocks_dev, BLOCK)
        incoming = lax.all_to_all(
            rounded[:, granted, :], ROWS, split_axis=1, concat_axis=1, tiled=True
        )
        sources = incoming[:, owner_dev, :]
        products = jnp.einsum(
            "ekj,kji->eki", sources, coupling_tiles, preferred_element_type=jnp.float32
        )
        coupled = jnp.einsum("eki,kb->ebi", products, placing, precision=highest)
        mixed_rows = (local_part + coupled).reshape(width_dev, rows_dev)
        fisher_dir = sum_at_owner(
            jnp.dot(
                width_factor, mixed_rows, precision=highest, preferred_element_type=jnp.float32
            ),
            "cols",
            0,
        )
        precond_fisher = precondition(fisher_dir)
        curvature, cross_term, second_term = (
            over_axes(jnp.sum(direction * fisher_dir), COLS_ROWS),
            over_axes(jnp.sum(fisher_dir * precond_res), COLS_ROWS),
            over_axes(jnp.sum(fisher_dir * precond_fisher), COLS_ROWS),
        )
        step_size = res_norm / curvature
        solution = solution + step_size * direction
        residual = residual - step_size * fisher_dir
        if iteration + 1 < ITERS:
            precond_res = precond_res - step_size * precond_fisher
            next_norm = (
                res_norm - 2.0 * step_size * cross_term + step_size * step_size * second_term
            )
            direction = precond_res + next_norm / res_norm * direction
            res_norm = next_norm
    return (solution, residual)


def solution(mesh):
    torus = Mesh(
        mesh.devices.reshape(mesh.shape["cols"], 8, 8, 2), ("cols", "rows_0", "rows_1", "rows_2")
    )
    placed = (
        P("cols", ROWS),
        P(None, "cols"),
        P(ROWS, None, None),
        P(ROWS, None, None),
        P(ROWS, None, None),
        P(ROWS),
        P(ROWS),
        P(ROWS),
    )
    return jax.shard_map(
        on_device,
        mesh=torus,
        in_specs=placed,
        out_specs=(P("cols", ROWS), P("cols", ROWS)),
        check_vma=False,
    )
```

profile of v0, /device:TPU:1, one launch (start us, length us, event | category | flops | bytes accessed | tf_op | source)
XLA Modules:
  0.0 713.6 jit_solution(2549009876126653616)
XLA Ops:
  3.0 18.4 %all-to-all-start = ((s32[128,1,1]{2,1,0:T(1,128)}), s32[128,1,1]{2,1,0:T(1,128)S(1)}, u32[]{:S(2)}, u32[]{:S(2)}) async-start(s32[128,1,1]{2,1,0:T(1,128)} %copy.150), calls=%async_computation | async-start | bytes 131072 | tf_op jit(solution)/shard_map/all_to_all | solution.py:58
  23.0 9.9 %all-to-all-done = s32[128,1,1]{2,1,0:T(1,128)S(1)} async-done(((s32[128,1,1]{2,1,0:T(1,128)}), s32[128,1,1]{2,1,0:T(1,128)S(1)}, u32[]{:S(2)}, u32[]{:S(2)}) %all-to-all-start) | async-done | bytes 544 | tf_op jit(solution)/shard_map/all_to_all | solution.py:58
  32.9 2.3 reduce.15
  37.0 5.7 all-to-all-start.1
  42.7 30.5 %all-to-all-done.1 = bf16[32,128,128]{2,0,1:T(8,128)(2,1)S(1)} async-done(((bf16[32,128,128]{2,0,1:T(8,128)(2,1)}), bf16[32,128,128]{2,0,1:T(8,128)(2,1)S(1)}, u32[]{:S(2)}, u32[]{:S(2)}) %all-to-all-start.1) | async-done | bytes 1048608 | tf_op jit(solution)/shard_map/all_to_all | solution.py:75
  79.5 4.3 all-to-all-start.2
  84.4 6.7 all-to-all-done.2
  94.0 7.6 %all-reduce.14 = (f32[]{:T(128)}, f32[]{:T(128)}, f32[]{:T(128)}) all-reduce(f32[]{:T(128)} %fusion.45, f32[]{:T(128)} %get-tuple-element.15, f32[]{:T(128)} %get-tuple-element.14), channel_id=1, replica_groups=mesh['cols'=4,'rows_0'=8,'rows_1'=8,'rows_2'=2] {'cols'}, use_global_device_ids=true, to_apply=%region_1.2 | all-reduce | flops 3 | bytes 24 | tf_op jit(solution)/shard_map/psum | solution.py:31
  101.7 15.3 %all-reduce.9 = (f32[]{:T(128)}, f32[]{:T(128)}, f32[]{:T(128)}) all-reduce(f32[]{:T(128)} %get-tuple-element.58, f32[]{:T(128)} %get-tuple-element.59, f32[]{:T(128)} %get-tuple-element.60), channel_id=1, replica_groups=mesh['cols'=4,'rows_0'=8,'rows_1'=8,'rows_2'=2] {'rows_0'}, use_global_device_ids=true, to_apply=%region_2.3 | all-reduce | flops 3 | bytes 24 | tf_op jit(solution)/shard_map/psum | solution.py:31
  117.0 11.4 %all-reduce.4 = (f32[]{:T(128)}, f32[]{:T(128)}, f32[]{:T(128)}) all-reduce(f32[]{:T(128)} %get-tuple-element.43, f32[]{:T(128)} %get-tuple-element.44, f32[]{:T(128)} %get-tuple-element.45), channel_id=1, replica_groups=mesh['cols'=4,'rows_0'=8,'rows_1'=8,'rows_2'=2] {'rows_1'}, use_global_device_ids=true, to_apply=%region_3.4 | all-reduce | flops 3 | bytes 24 | tf_op jit(solution)/shard_map/psum | solution.py:31
  128.3 13.9 %all-reduce.19 = (f32[]{:T(128)}, f32[]{:T(128)}, f32[]{:T(128)}) all-reduce(f32[]{:T(128)} %get-tuple-element.28, f32[]{:T(128)} %get-tuple-element.29, f32[]{:T(128)} %get-tuple-element.30), channel_id=1, replica_groups=mesh['cols'=4,'rows_0'=8,'rows_1'=8,'rows_2'=2] {'rows_2'}, use_global_device_ids=true, to_apply=%region_4.5 | all-reduce | flops 3 | bytes 24 | tf_op jit(solution)/shard_map/psum | solution.py:31
  148.9 39.0 %all_to_all.72 = bf16[32,128,128]{2,0,1:T(8,128)(2,1)} all-to-all(bf16[32,128,128]{2,0,1:T(8,128)(2,1)} %bitcast.331), channel_id=1, replica_groups=mesh['cols'=4,'rows_0'=8,'rows_1'=8,'rows_2'=2] {'rows_0','rows_1','rows..., dimensions={1} | all-to-all | bytes 2097152 | tf_op jit(solution)/shard_map/all_to_all | solution.py:75
  187.9 2.7 gather_fusion.3
  194.5 10.8 %all_to_all.73 = f32[4,32,1024]{2,1,0:T(8,128)} all-to-all(f32[4,32,1024]{2,1,0:T(8,128)S(1)} %bitcast.336), channel_id=1, replica_groups=mesh['cols'=4,'rows_0'=8,'rows_1'=8,'rows_2'=2] {'cols'}, dimensions={0} | all-to-all | bytes 1048576 | tf_op jit(solution)/shard_map/all_to_all | solution.py:26
  210.9 7.6 %all-reduce.13 = (f32[]{:T(128)}, f32[]{:T(128)}, f32[]{:T(128)}) all-reduce(f32[]{:T(128)} %get-tuple-element.13, f32[]{:T(128)} %get-tuple-element.12, f32[]{:T(128)} %get-tuple-element.11), channel_id=1, replica_groups=mesh['cols'=4,'rows_0'=8,'rows_1'=8,'rows_2'=2] {'cols'}, use_global_device_ids=true, to_apply=%region_19.20 | all-reduce | flops 3 | bytes 24 | tf_op jit(solution)/shard_map/psum | solution.py:31
  218.4 15.0 %all-reduce.8 = (f32[]{:T(128)}, f32[]{:T(128)}, f32[]{:T(128)}) all-reduce(f32[]{:T(128)} %get-tuple-element.55, f32[]{:T(128)} %get-tuple-element.56, f32[]{:T(128)} %get-tuple-element.57), channel_id=1, replica_groups=mesh['cols'=4,'rows_0'=8,'rows_1'=8,'rows_2'=2] {'rows_0'}, use_global_device_ids=true, to_apply=%region_20.21 | all-reduce | flops 3 | bytes 24 | tf_op jit(solution)/shard_map/psum | solution.py:31
  233.5 11.4 %all-reduce.3 = (f32[]{:T(128)}, f32[]{:T(128)}, f32[]{:T(128)}) all-reduce(f32[]{:T(128)} %get-tuple-element.40, f32[]{:T(128)} %get-tuple-element.41, f32[]{:T(128)} %get-tuple-element.42), channel_id=1, replica_groups=mesh['cols'=4,'rows_0'=8,'rows_1'=8,'rows_2'=2] {'rows_1'}, use_global_device_ids=true, to_apply=%region_21.22 | all-reduce | flops 3 | bytes 24 | tf_op jit(solution)/shard_map/psum | solution.py:31
  244.9 13.5 %all-reduce.18 = (f32[]{:T(128)}, f32[]{:T(128)}, f32[]{:T(128)}) all-reduce(f32[]{:T(128)} %get-tuple-element.25, f32[]{:T(128)} %get-tuple-element.26, f32[]{:T(128)} %get-tuple-element.27), channel_id=1, replica_groups=mesh['cols'=4,'rows_0'=8,'rows_1'=8,'rows_2'=2] {'rows_2'}, use_global_device_ids=true, to_apply=%region_22.23 | all-reduce | flops 3 | bytes 24 | tf_op jit(solution)/shard_map/psum | solution.py:31
  263.8 39.1 %all_to_all.74 = bf16[32,128,128]{2,0,1:T(8,128)(2,1)} all-to-all(bf16[32,128,128]{2,0,1:T(8,128)(2,1)} %bitcast.332), channel_id=1, replica_groups=mesh['cols'=4,'rows_0'=8,'rows_1'=8,'rows_2'=2] {'rows_0','rows_1','rows..., dimensions={1} | all-to-all | bytes 2097152 | tf_op jit(solution)/shard_map/all_to_all | solution.py:75
  302.9 2.7 gather_fusion.5
  309.5 10.8 %all_to_all.75 = f32[4,32,1024]{2,1,0:T(8,128)} all-to-all(f32[4,32,1024]{2,1,0:T(8,128)S(1)} %bitcast.337), channel_id=1, replica_groups=mesh['cols'=4,'rows_0'=8,'rows_1'=8,'rows_2'=2] {'cols'}, dimensions={0} | all-to-all | bytes 1048576 | tf_op jit(solution)/shard_map/all_to_all | solution.py:26
  322.1 2.9 fusion.63
  325.0 7.6 %all-reduce.12 = (f32[]{:T(128)}, f32[]{:T(128)}, f32[]{:T(128)}) all-reduce(f32[]{:T(128)} %get-tuple-element.10, f32[]{:T(128)} %get-tuple-element.9, f32[]{:T(128)} %get-tuple-element.8), channel_id=1, replica_groups=mesh['cols'=4,'rows_0'=8,'rows_1'=8,'rows_2'=2] {'cols'}, use_global_device_ids=true, to_apply=%region_35.36 | all-reduce | flops 3 | bytes 24 | tf_op jit(solution)/shard_map/psum | solution.py:31
  332.5 15.1 %all-reduce.7 = (f32[]{:T(128)}, f32[]{:T(128)}, f32[]{:T(128)}) all-reduce(f32[]{:T(128)} %get-tuple-element.52, f32[]{:T(128)} %get-tuple-element.53, f32[]{:T(128)} %get-tuple-element.54), channel_id=1, replica_groups=mesh['cols'=4,'rows_0'=8,'rows_1'=8,'rows_2'=2] {'rows_0'}, use_global_device_ids=true, to_apply=%region_36.37 | all-reduce | flops 3 | bytes 24 | tf_op jit(solution)/shard_map/psum | solution.py:31
  347.6 11.7 %all-reduce.2 = (f32[]{:T(128)}, f32[]{:T(128)}, f32[]{:T(128)}) all-reduce(f32[]{:T(128)} %get-tuple-element.37, f32[]{:T(128)} %get-tuple-element.38, f32[]{:T(128)} %get-tuple-element.39), channel_id=1, replica_groups=mesh['cols'=4,'rows_0'=8,'rows_1'=8,'rows_2'=2] {'rows_1'}, use_global_device_ids=true, to_apply=%region_37.38 | all-reduce | flops 3 | bytes 24 | tf_op jit(solution)/shard_map/psum | solution.py:31
  359.3 13.2 %all-reduce.17 = (f32[]{:T(128)}, f32[]{:T(128)}, f32[]{:T(128)}) all-reduce(f32[]{:T(128)} %get-tuple-element.22, f32[]{:T(128)} %get-tuple-element.23, f32[]{:T(128)} %get-tuple-element.24), channel_id=1, replica_groups=mesh['cols'=4,'rows_0'=8,'rows_1'=8,'rows_2'=2] {'rows_2'}, use_global_device_ids=true, to_apply=%region_38.39 | all-reduce | flops 3 | bytes 24 | tf_op jit(solution)/shard_map/psum | solution.py:31
  377.9 39.1 %all_to_all.76 = bf16[32,128,128]{2,0,1:T(8,128)(2,1)} all-to-all(bf16[32,128,128]{2,0,1:T(8,128)(2,1)} %bitcast.333), channel_id=1, replica_groups=mesh['cols'=4,'rows_0'=8,'rows_1'=8,'rows_2'=2] {'rows_0','rows_1','rows..., dimensions={1} | all-to-all | bytes 2097152 | tf_op jit(solution)/shard_map/all_to_all | solution.py:75
  417.0 2.7 gather_fusion.7
  423.7 10.8 %all_to_all.77 = f32[4,32,1024]{2,1,0:T(8,128)} all-to-all(f32[4,32,1024]{2,1,0:T(8,128)S(1)} %bitcast.338), channel_id=1, replica_groups=mesh['cols'=4,'rows_0'=8,'rows_1'=8,'rows_2'=2] {'cols'}, dimensions={0} | all-to-all | bytes 1048576 | tf_op jit(solution)/shard_map/all_to_all | solution.py:26
  436.2 2.9 fusion.59
  439.1 7.6 %all-reduce.11 = (f32[]{:T(128)}, f32[]{:T(128)}, f32[]{:T(128)}) all-reduce(f32[]{:T(128)} %get-tuple-element.7, f32[]{:T(128)} %get-tuple-element.6, f32[]{:T(128)} %get-tuple-element.5), channel_id=1, replica_groups=mesh['cols'=4,'rows_0'=8,'rows_1'=8,'rows_2'=2] {'cols'}, use_global_device_ids=true, to_apply=%region_51.52 | all-reduce | flops 3 | bytes 24 | tf_op jit(solution)/shard_map/psum | solution.py:31
  446.7 15.0 %all-reduce.6 = (f32[]{:T(128)}, f32[]{:T(128)}, f32[]{:T(128)}) all-reduce(f32[]{:T(128)} %get-tuple-element.49, f32[]{:T(128)} %get-tuple-element.50, f32[]{:T(128)} %get-tuple-element.51), channel_id=1, replica_groups=mesh['cols'=4,'rows_0'=8,'rows_1'=8,'rows_2'=2] {'rows_0'}, use_global_device_ids=true, to_apply=%region_52.53 | all-reduce | flops 3 | bytes 24 | tf_op jit(solution)/shard_map/psum | solution.py:31
  461.7 11.4 %all-reduce.1 = (f32[]{:T(128)}, f32[]{:T(128)}, f32[]{:T(128)}) all-reduce(f32[]{:T(128)} %get-tuple-element.34, f32[]{:T(128)} %get-tuple-element.35, f32[]{:T(128)} %get-tuple-element.36), channel_id=1, replica_groups=mesh['cols'=4,'rows_0'=8,'rows_1'=8,'rows_2'=2] {'rows_1'}, use_global_device_ids=true, to_apply=%region_53.54 | all-reduce | flops 3 | bytes 24 | tf_op jit(solution)/shard_map/psum | solution.py:31
  473.1 13.5 %all-reduce.16 = (f32[]{:T(128)}, f32[]{:T(128)}, f32[]{:T(128)}) all-reduce(f32[]{:T(128)} %get-tuple-element.19, f32[]{:T(128)} %get-tuple-element.20, f32[]{:T(128)} %get-tuple-element.21), channel_id=1, replica_groups=mesh['cols'=4,'rows_0'=8,'rows_1'=8,'rows_2'=2] {'rows_2'}, use_global_device_ids=true, to_apply=%region_54.55 | all-reduce | flops 3 | bytes 24 | tf_op jit(solution)/shard_map/psum | solution.py:31
  492.0 39.1 %all_to_all.78 = bf16[32,128,128]{2,0,1:T(8,128)(2,1)} all-to-all(bf16[32,128,128]{2,0,1:T(8,128)(2,1)} %bitcast.334), channel_id=1, replica_groups=mesh['cols'=4,'rows_0'=8,'rows_1'=8,'rows_2'=2] {'rows_0','rows_1','rows..., dimensions={1} | all-to-all | bytes 2097152 | tf_op jit(solution)/shard_map/all_to_all | solution.py:75
  531.1 2.7 gather_fusion.9
  537.8 10.8 %all_to_all.79 = f32[4,32,1024]{2,1,0:T(8,128)} all-to-all(f32[4,32,1024]{2,1,0:T(8,128)S(1)} %bitcast.339), channel_id=1, replica_groups=mesh['cols'=4,'rows_0'=8,'rows_1'=8,'rows_2'=2] {'cols'}, dimensions={0} | all-to-all | bytes 1048576 | tf_op jit(solution)/shard_map/all_to_all | solution.py:26
  549.7 2.8 fusion.55
  552.5 7.6 %all-reduce.10 = (f32[]{:T(128)}, f32[]{:T(128)}, f32[]{:T(128)}) all-reduce(f32[]{:T(128)} %get-tuple-element.4, f32[]{:T(128)} %get-tuple-element.3, f32[]{:T(128)} %get-tuple-element.2), channel_id=1, replica_groups=mesh['cols'=4,'rows_0'=8,'rows_1'=8,'rows_2'=2] {'cols'}, use_global_device_ids=true, to_apply=%region_67.68 | all-reduce | flops 3 | bytes 24 | tf_op jit(solution)/shard_map/psum | solution.py:31
  560.1 15.1 %all-reduce.5 = (f32[]{:T(128)}, f32[]{:T(128)}, f32[]{:T(128)}) all-reduce(f32[]{:T(128)} %get-tuple-element.46, f32[]{:T(128)} %get-tuple-element.47, f32[]{:T(128)} %get-tuple-element.48), channel_id=1, replica_groups=mesh['cols'=4,'rows_0'=8,'rows_1'=8,'rows_2'=2] {'rows_0'}, use_global_device_ids=true, to_apply=%region_68.69 | all-reduce | flops 3 | bytes 24 | tf_op jit(solution)/shard_map/psum | solution.py:31
  575.2 11.4 %all-reduce = (f32[]{:T(128)}, f32[]{:T(128)}, f32[]{:T(128)}) all-reduce(f32[]{:T(128)} %get-tuple-element.31, f32[]{:T(128)} %get-tuple-element.32, f32[]{:T(128)} %get-tuple-element.33), channel_id=1, replica_groups=mesh['cols'=4,'rows_0'=8,'rows_1'=8,'rows_2'=2] {'rows_1'}, use_global_device_ids=true, to_apply=%region_69.70 | all-reduce | flops 3 | bytes 24 | tf_op jit(solution)/shard_map/psum | solution.py:31
  586.6 13.5 %all-reduce.15 = (f32[]{:T(128)}, f32[]{:T(128)}, f32[]{:T(128)}) all-reduce(f32[]{:T(128)} %get-tuple-element.16, f32[]{:T(128)} %get-tuple-element.17, f32[]{:T(128)} %get-tuple-element.18), channel_id=1, replica_groups=mesh['cols'=4,'rows_0'=8,'rows_1'=8,'rows_2'=2] {'rows_2'}, use_global_device_ids=true, to_apply=%region_70.71 | all-reduce | flops 3 | bytes 24 | tf_op jit(solution)/shard_map/psum | solution.py:31
  605.5 39.1 %all_to_all.80 = bf16[32,128,128]{2,0,1:T(8,128)(2,1)} all-to-all(bf16[32,128,128]{2,0,1:T(8,128)(2,1)} %bitcast.330), channel_id=1, replica_groups=mesh['cols'=4,'rows_0'=8,'rows_1'=8,'rows_2'=2] {'rows_0','rows_1','rows..., dimensions={1} | all-to-all | bytes 2097152 | tf_op jit(solution)/shard_map/all_to_all | solution.py:75
  649.5 10.2 %all_to_all.81 = f32[4,32,1024]{2,1,0:T(8,128)S(1)} all-to-all(f32[4,32,1024]{2,1,0:T(8,128)S(1)} %bitcast.340), channel_id=1, replica_groups=mesh['cols'=4,'rows_0'=8,'rows_1'=8,'rows_2'=2] {'cols'}, dimensions={0} | all-to-all | bytes 1048576 | tf_op jit(solution)/shard_map/all_to_all | solution.py:26
  661.3 7.5 %psum.520 = f32[]{:T(128)} all-reduce(f32[]{:T(128)} %fusion.51), channel_id=1, replica_groups=mesh['cols'=4,'rows_0'=8,'rows_1'=8,'rows_2'=2] {'cols'}, use_global_device_ids=true, to_apply=%region_83.84 | all-reduce | flops 1 | bytes 8 | tf_op jit(solution)/shard_map/psum | solution.py:31
  668.8 15.1 %psum.521 = f32[]{:T(128)} all-reduce(f32[]{:T(128)} %psum.520), channel_id=1, replica_groups=mesh['cols'=4,'rows_0'=8,'rows_1'=8,'rows_2'=2] {'rows_0'}, use_global_device_ids=true, to_apply=%region_84.85 | all-reduce | flops 1 | bytes 8 | tf_op jit(solution)/shard_map/psum | solution.py:31
  683.9 11.4 %psum.522 = f32[]{:T(128)} all-reduce(f32[]{:T(128)} %psum.521), channel_id=1, replica_groups=mesh['cols'=4,'rows_0'=8,'rows_1'=8,'rows_2'=2] {'rows_1'}, use_global_device_ids=true, to_apply=%region_85.86 | all-reduce | flops 1 | bytes 8 | tf_op jit(solution)/shard_map/psum | solution.py:31
  695.2 13.5 %psum.523 = f32[]{:T(128)} all-reduce(f32[]{:T(128)} %psum.522), channel_id=1, replica_groups=mesh['cols'=4,'rows_0'=8,'rows_1'=8,'rows_2'=2] {'rows_2'}, use_global_device_ids=true, to_apply=%region_86.87 | all-reduce | flops 1 | bytes 8 | tf_op jit(solution)/shard_map/psum | solution.py:31
  (106 shorter events, 67.5 us)
Async XLA Ops:
  0.6 74.0 %copy-start = (bf16[64,128,128]{2,1,0:T(8,128)(2,1)S(1)}, bf16[64,128,128]{2,1,0:T(8,128)(2,1)}, u32[]{:S(2)}) copy-start(bf16[64,128,128]{2,1,0:T(8,128)(2,1)} %param.12) | copy-start | bytes 6291460
  1.5 74.9 %copy-start.14 = (pred[64]{0:T(512)(128)(4,1)}, pred[64]{0:T(512)(128)(4,1)S(1)}, u32[]{:S(2)}) copy-start(pred[64]{0:T(512)(128)(4,1)S(1)} %iota_compare_fusion.2) | copy-start | bytes 196
  3.0 29.9 %all-to-all-start = ((s32[128,1,1]{2,1,0:T(1,128)}), s32[128,1,1]{2,1,0:T(1,128)S(1)}, u32[]{:S(2)}, u32[]{:S(2)}) async-start(s32[128,1,1]{2,1,0:T(1,128)} %copy.150), calls=%async_computation | async-start | bytes 131072 | tf_op jit(solution)/shard_map/all_to_all | solution.py:58
  35.3 1.7 copy-start.20
  37.0 36.2 %all-to-all-start.1 = ((bf16[32,128,128]{2,0,1:T(8,128)(2,1)}), bf16[32,128,128]{2,0,1:T(8,128)(2,1)S(1)}, u32[]{:S(2)}, u32[]{:S(2)}) async-start(bf16[32,128,128]{2,0,1:T(8,128)(2,1)} %bitcast.5), calls=%async_computation.1 | async-start | bytes 2097152 | tf_op jit(solution)/shard_map/all_to_all | solution.py:75
  42.7 31.9 %copy-start.22 = (s32[1024]{0:T(1024)}, s32[1024]{0:T(1024)S(1)}, u32[]{:S(2)}) copy-start(s32[1024]{0:T(1024)S(1)} %pad_clamp_fusion) | copy-start | bytes 12292
  74.6 1.8 copy-start.17
  74.6 2.8 copy-start.1
  74.6 3.4 copy-start.13
  76.4 7.3 %copy-start.9 = (f32[32,1024]{1,0:T(8,128)S(1)}, f32[32,1024]{1,0:T(8,128)}, u32[]{:S(2)}) copy-start(f32[32,1024]{1,0:T(8,128)} %param.8) | copy-start | bytes 393220
  76.4 15.7 %copy-start.2 = (f32[8,128,128]{2,1,0:T(8,128)S(1)}, f32[8,128,128]{2,1,0:T(8,128)}, u32[]{:S(2)}) copy-start(f32[8,128,128]{2,1,0:T(8,128)} %param.11) | copy-start | bytes 1572868
  79.5 67.7 %copy-start.21 = (s32[1024]{0:T(1024)S(1)}, s32[1024]{0:T(1024)}, u32[]{:S(2)}) copy-start(s32[1024]{0:T(1024)} %copy-done.20) | copy-start | bytes 12292
  79.5 11.6 %all-to-all-start.2 = ((f32[4,32,1024]{2,1,0:T(8,128)}), f32[4,32,1024]{2,1,0:T(8,128)}, u32[]{:S(2)}, u32[]{:S(2)}) async-start(f32[4,32,1024]{2,1,0:T(8,128)} %bitcast.335), calls=%async_computation.2 | async-start | bytes 1048576 | tf_op jit(solution)/shard_map/all_to_all | solution.py:26
  92.1 54.1 %copy-start.11 = (f32[32,1024]{1,0:T(8,128)}, f32[32,1024]{1,0:T(8,128)S(1)}, u32[]{:S(2)}) copy-start(f32[32,1024]{1,0:T(8,128)S(1)} %reduce_sum.225) | copy-start | bytes 393220
  147.1 61.4 %copy-start.3 = (f32[32,8,128]{2,0,1:T(8,128)}, f32[32,8,128]{2,0,1:T(8,128)S(1)}, u32[]{:S(2)}) copy-start(f32[32,8,128]{2,0,1:T(8,128)S(1)} %get-tuple-element.88) | copy-start | bytes 393220
  147.2 40.7 %copy-start.23 = (s32[1024]{0:T(1024)S(1)}, s32[1024]{0:T(1024)}, u32[]{:S(2)}) copy-start(s32[1024]{0:T(1024)} %copy-done.22) | copy-start | bytes 12292
  190.5 1.7 copy-start.15
  190.5 1.7 copy-start.18
  208.5 2.3 copy-start.12
  419.7 2.8 copy-start.4
  533.8 2.8 copy-start.5
  549.7 94.9 %copy-start.8 = (f32[32,1024]{1,0:T(8,128)}, f32[32,1024]{1,0:T(8,128)S(1)}, u32[]{:S(2)}) copy-start(f32[32,1024]{1,0:T(8,128)S(1)} %reduce_sum.244) | copy-start | bytes 393220
  646.5 0.7 copy-start.16
  646.6 0.7 copy-start.19
  646.6 1.7 copy-start.10
  647.2 62.2 %copy-start.6 = (f32[32,1024]{1,0:T(8,128)S(1)}, f32[32,1024]{1,0:T(8,128)}, u32[]{:S(2)}) copy-start(f32[32,1024]{1,0:T(8,128)} %reduce_sum.229) | copy-start | bytes 393220
  647.3 62.2 %copy-start.7 = (f32[32,1024]{1,0:T(8,128)S(1)}, f32[32,1024]{1,0:T(8,128)}, u32[]{:S(2)}) copy-start(f32[32,1024]{1,0:T(8,128)} %reduce_sum.234) | copy-start | bytes 393220
where the time goes:
time: 724 us; the launch traced here: 714 us
  blocking collectives  535 us (74%)
  waiting for transfers between devices  47 us (6%)
  matrix products  37 us (5%)
  starting transfers between devices  28.4 us (4%)
  other arithmetic  26.8 us (4%)
  local copies, waits for them, and re-layouts  25.3 us (3%)
  between operations  14.6 us (2%)
    psum x24, blocking collectives, over_axes(): return functools.reduce(lax.psum, axes, array)  286 us
    all_to_all x5, blocking collectives, on_device(): lax.all_to_all(rounded[:, granted, :], ROWS, split_axis=1, concat_axis=1,...  195 us
    all_to_all x5, blocking collectives, sum_at_owner(): lax.all_to_all(pieces, axis, split_axis=0, concat_axis=0, tiled=True)  53.5 us
    all_to_all x1, waiting for transfers between devices, on_device(): lax.all_to_all(rounded[:, granted, :], ROWS, split_axis=1, concat_axis=1,...  30.5 us
    all_to_all x1, starting transfers between devices, on_device(): lax.all_to_all(request, ROWS, split_axis=0, concat_axis=0, tiled=True)  18.4 us
  transfers between devices with their start and end apart: 3, of which 3 were waited for; matrix products, arithmetic and copies ran while one was open for 0% of the time, Pallas kernels for 0%

commit v1 on v0

v1 whole, which is shorter than its diff:
```python
import functools
import math

import jax
import jax.numpy as jnp
from jax import lax
from jax.experimental import pallas as pl
from jax.experimental.pallas import tpu as pltpu
from jax.sharding import PartitionSpec as P

BLOCK = 128
ITERS = 6
BLOCKS_DEV = 8
MESH = pl.DeviceIdType.MESH
f32, bf16 = jnp.float32, jnp.bfloat16


def dot(a, b):
    return jnp.dot(a, b, preferred_element_type=f32)


def split(v):
    high = v.astype(bf16)
    return high, (v - high.astype(f32)).astype(bf16)


def times_tile(v, high_ref, low_ref, n):
    width = v.shape[0]
    high, low = split(v)
    both = dot(jnp.concatenate([high, low], axis=0), high_ref[n])
    return both[:width] + both[width:] + dot(high, low_ref[n])


def kernel(
    nx, side, slots, width,
    local_s, remote_s, count_s, grad_ref, wt_ref, diag_ref, jac_ref, tiles_ref,
    sol_ref, res_ref,
    r, z, d, q, gz, xs, err, t, terr,
    jh, jl, dh, dl, wstack, wh, scal,
    grant_row, grant_got, grant_s, index0_s, index1_s, place_s,
    ag_snd, ag_even_y, ag_even_z, ag_odd_y, ag_odd_z,
    aa_snd, aa_even_y, aa_even_z, aa_odd_y, aa_odd_z, xd_snd, xd_got, xc_snd, xc_got,
    ra_snd, ra_got, rb_snd, rb_got, rc_snd, rc_got,
    g_ssem, g_rsem, g_csem, ag_ssem, ag_rsem, aa_ssem, aa_rsem, xd_ssem, xd_rsem,
    xc_ssem, xc_rsem, r_ssem, r_rsem,
):
    ag_got = ((ag_even_y, ag_even_z), (ag_odd_y, ag_odd_z))
    aa_got = ((aa_even_y, aa_even_z), (aa_odd_y, aa_odd_z))
    blocks = BLOCKS_DEV
    half = width // 2
    ring = 2 * side
    mx = lax.axis_index("cols")
    me = lax.axis_index("rows")
    y, zc = me // ring, me % ring
    zz, c = zc // 2, me % 2
    yc = y * 2 + c

    def along_y(i):
        return i * ring + zc

    def along_z(i):
        return y * ring + i * 2 + c

    def in_zc(i):
        return y * ring + i

    def in_yc(i):
        return (i // 2) * ring + zz * 2 + i % 2

    def push(src, dst, ssem, rsem, device):
        pltpu.make_async_remote_copy(
            src_ref=src, dst_ref=dst, send_sem=ssem, recv_sem=rsem,
            device_id=device, device_id_type=MESH,
        ).start()

    def await_sent(ref, sem):
        pltpu.make_async_remote_copy(
            src_ref=ref, dst_ref=ref, send_sem=sem, recv_sem=sem,
            device_id={"rows": me}, device_id_type=MESH,
        ).wait_send()

    def await_got(ref, sem):
        pltpu.make_async_remote_copy(
            src_ref=ref, dst_ref=ref, send_sem=sem, recv_sem=sem,
            device_id={"rows": me}, device_id_type=MESH,
        ).wait_recv()

    barrier = pltpu.get_barrier_semaphore()
    partners = 0
    for j in range(1, ring):
        pl.semaphore_signal(
            barrier, inc=1, device_id={"rows": in_zc((zc + j) % ring)}, device_id_type=MESH
        )
        partners += 1
    for j in range(1, side):
        for k in range(2):
            pl.semaphore_signal(
                barrier, inc=1, device_id={"rows": in_yc(((y + j) % side) * 2 + k)},
                device_id_type=MESH,
            )
            partners += 1
    for j in range(1, nx):
        pl.semaphore_signal(
            barrier, inc=1, device_id={"cols": (mx + j) % nx}, device_id_type=MESH
        )
        partners += 1

    lanes = lax.broadcasted_iota(jnp.int32, (1, 128), 1)
    row = jnp.zeros((1, 128), jnp.int32)
    count = count_s[0]
    for k in range(slots):
        live = k < count
        local = local_s[k]
        owner = remote_s[k] // blocks
        row = jnp.where(lanes == jnp.where(live, owner, -1), local, row)
        oy, ozc = owner // ring, owner % ring
        index0_s[k] = ozc * side + oy
        index1_s[k] = (oy * 2 + owner % 2) * side + ozc // 2
        placed = jnp.where(live, local, blocks)
        for n in range(blocks):
            place_s[k * blocks + n] = jnp.where(placed == n, 1.0, 0.0).astype(f32)
    grant_row[...] = row

    for n in range(blocks):
        high, low = split(jac_ref[n])
        jh[n] = high
        jl[n] = low
        high, low = split(diag_ref[n])
        dh[n] = high
        dl[n] = low
        start = grad_ref[:, n * BLOCK : (n + 1) * BLOCK]
        r[n] = start
        q[n] = start
        for ref in (z, d, gz, xs, err):
            ref[n] = jnp.zeros((width, BLOCK), f32)
    high, low = split(wt_ref[...])
    wh[...] = high
    wstack[...] = jnp.concatenate([high, low], axis=0)
    scal[...] = jnp.zeros((8, 128), f32)

    pl.semaphore_wait(barrier, partners)

    for j in range(1, side):
        i = (y + j) % side
        push(grant_row, grant_got.at[0, y], g_ssem.at[0], g_rsem.at[0], {"rows": along_y(i)})
        i = (zz + j) % side
        push(grant_row, grant_got.at[1, zz], g_ssem.at[1], g_rsem.at[1], {"rows": along_z(i)})
    grant_got[0, y] = row
    grant_got[1, zz] = row

    def sums(e_par, values):
        ra_snd[...] = values
        ra_got[e_par, zc] = values
        for j in range(1, ring):
            push(ra_snd, ra_got.at[e_par, zc], r_ssem.at[0], r_rsem.at[0, e_par],
                 {"rows": in_zc((zc + j) % ring)})

    def sums_y(e_par):
        await_got(ra_got.at[e_par, pl.ds(0, ring - 1)], r_rsem.at[0, e_par])
        total = ra_got[e_par, 0]
        for i in range(1, ring):
            total = total + ra_got[e_par, i]
        rb_snd[...] = total
        rb_got[e_par, y] = total
        for j in range(1, side):
            push(rb_snd, rb_got.at[e_par, y], r_ssem.at[1], r_rsem.at[1, e_par],
                 {"rows": along_y((y + j) % side)})

    def sums_x(e_par):
        await_got(rb_got.at[e_par, pl.ds(0, side - 1)], r_rsem.at[1, e_par])
        total = rb_got[e_par, 0]
        for i in range(1, side):
            total = total + rb_got[e_par, i]
        rc_snd[...] = total
        rc_got[e_par, mx] = total
        for j in range(1, nx):
            push(rc_snd, rc_got.at[e_par, mx], r_ssem.at[2], r_rsem.at[2, e_par],
                 {"cols": (mx + j) % nx})

    def sums_end(e_par):
        await_got(rc_got.at[e_par, pl.ds(0, nx - 1)], r_rsem.at[2, e_par])
        total = rc_got[e_par, 0]
        for i in range(1, nx):
            total = total + rc_got[e_par, i]
        await_sent(ra_got.at[e_par, pl.ds(0, ring - 1)], r_ssem.at[0])
        await_sent(rb_got.at[e_par, pl.ds(0, side - 1)], r_ssem.at[1])
        await_sent(rc_got.at[e_par, pl.ds(0, nx - 1)], r_ssem.at[2])
        lane_sum = jnp.sum(total, axis=1, keepdims=True)
        return jnp.broadcast_to(lane_sum, (8, 128))

    def inner(pairs):
        rows = []
        for a, b in pairs:
            part = jnp.zeros((8, 128), f32)
            for n in range(blocks):
                prod = a[n] * b[n]
                for s in range(0, width, 8):
                    part = part + prod[s : s + 8]
            rows.append(jnp.sum(part, axis=0, keepdims=True))
        rows.append(jnp.zeros((8 - len(rows), 128), f32))
        return jnp.concatenate(rows, axis=0)

    def step(e, par):
        first = e == 0
        scales = scal[...]
        norm, inverse = scales[0:1], scales[1:2]

        for n in range(blocks):
            tn = times_tile(q[n], jh, jl, n)
            t[n] = tn
            msg = (tn + err[n] * inverse).astype(bf16)
            terr[n] = msg.astype(f32) - tn
            ag_snd[0, n] = msg[:half]
            ag_snd[1, n] = msg[half:]
            ag_got[par][0][y, n] = msg[:half]
            ag_got[par][1][zz, n] = msg[half:]
        for j in range(1, side):
            push(ag_snd.at[0], ag_got[par][0].at[y], ag_ssem.at[0], ag_rsem.at[0, par],
                 {"rows": along_y((y + j) % side)})
            push(ag_snd.at[1], ag_got[par][1].at[zz], ag_ssem.at[1], ag_rsem.at[1, par],
                 {"rows": along_z((zz + j) % side)})

        sums(par, inner([(d, q), (q, z), (q, t)]))

        for n in range(blocks):
            part = times_tile(t[n], dh, dl, n)
            xd_snd[n] = part
            xd_got[par, mx, n] = part
        for j in range(1, nx):
            push(xd_snd, xd_got.at[par, mx], xd_ssem, xd_rsem.at[par], {"cols": (mx + j) % nx})

        sums_y(par)

        for o in range(2):
            await_got(ag_got[par][o].at[pl.ds(0, side - 1)], ag_rsem.at[o, par])
            for i in range(ring):
                column = in_zc(i) if o == 0 else in_yc(i)
                for s in range(side):
                    aa_snd[o, i, s] = ag_got[par][o][s, grant_s[o, s, 0, column]]
            mine = zc if o == 0 else yc
            for j in range(1, ring):
                i = (mine + j) % ring
                push(aa_snd.at[o, i], aa_got[par][o].at[pl.ds(mine * side, side)],
                     aa_ssem.at[o], aa_rsem.at[o, par],
                     {"rows": in_zc(i) if o == 0 else in_yc(i)})
            for s in range(side):
                aa_got[par][o][mine * side + s] = aa_snd[o, mine, s]

        sums_x(par)
        total = sums_end(par)
        curvature, cross, second = total[0:1], total[1:2], total[2:3]
        size = norm / curvature
        following = norm - 2.0 * size * cross + size * size * second
        a = jnp.where(first, -1.0, size)
        a_res = jnp.where(first, 0.0, size)
        b = jnp.where(first, 0.0, following / norm)
        scal[0:1] = jnp.where(first, second, following)
        scal[1:2] = jnp.where(first, 0.0, 1.0 / a)
        for n in range(blocks):
            dn = d[n]
            xs[n] = xs[n] + a * dn
            r[n] = r[n] - a_res * q[n]
            zn = z[n] - a * t[n]
            z[n] = zn
            d[n] = zn + b * dn
            err[n] = err[n] - a * terr[n]

        for o in range(2):
            await_got(aa_got[par][o].at[pl.ds(0, (ring - 1) * side)], aa_rsem.at[o, par])

        unroll = 16

        def tiles(group, sums_of):
            sums_of = list(sums_of)
            for u in range(unroll):
                k = group * unroll + u
                source = jnp.concatenate(
                    [aa_got[par][0][index0_s[k]], aa_got[par][1][index1_s[k]]], axis=0
                )
                prod = dot(source, tiles_ref[k])
                for n in range(blocks):
                    sums_of[n] = sums_of[n] + place_s[k * blocks + n] * prod
            return tuple(sums_of)

        zero = jnp.zeros((width, BLOCK), f32)
        coupled = lax.fori_loop(0, slots // unroll, tiles, (zero,) * blocks)
        for n in range(blocks):
            part = coupled[n].astype(bf16)
            xc_snd[n] = part
            xc_got[par, mx, n] = part
        for j in range(1, nx):
            push(xc_snd, xc_got.at[par, mx], xc_ssem, xc_rsem.at[par], {"cols": (mx + j) % nx})
        await_got(xd_got.at[par, pl.ds(0, nx - 1)], xd_rsem.at[par])
        await_got(xc_got.at[par, pl.ds(0, nx - 1)], xc_rsem.at[par])

        for n in range(blocks):
            mixed = jnp.concatenate(
                [xd_got[par, i, n] + xc_got[par, i, n].astype(f32) for i in range(nx)], axis=0
            )
            high, low = split(mixed)
            both = dot(wstack[...], high)
            image = both[:width] + both[width:] + dot(wh[...], low)
            gn = gz[n] - a * image
            gz[n] = gn
            q[n] = gn + b * q[n]

        for o in range(2):
            await_sent(ag_got[par][o].at[pl.ds(0, side - 1)], ag_ssem.at[o])
            await_sent(aa_got[par][o].at[pl.ds(0, (ring - 1) * side)], aa_ssem.at[o])
        await_sent(xd_got.at[par, pl.ds(0, nx - 1)], xd_ssem)
        await_sent(xc_got.at[par, pl.ds(0, nx - 1)], xc_ssem)

    for o in range(2):
        await_got(grant_got.at[o, pl.ds(0, side - 1)], g_rsem.at[o])
        await_sent(grant_got.at[o, pl.ds(0, side - 1)], g_ssem.at[o])
    tables = pltpu.make_async_copy(grant_got, grant_s, g_csem)
    tables.start()
    tables.wait()

    def two_steps(i, carry):
        step(2 * i, 0)
        step(2 * i + 1, 1)
        return carry

    lax.fori_loop(0, ITERS // 2, two_steps, 0)

    par = ITERS % 2
    sums(par, inner([(d, q)]))
    sums_y(par)
    sums_x(par)
    total = sums_end(par)
    a = scal[0:1] / total[0:1]
    for n in range(blocks):
        sol_ref[:, n * BLOCK : (n + 1) * BLOCK] = xs[n] + a * d[n]
        res_ref[:, n * BLOCK : (n + 1) * BLOCK] = r[n] - a * q[n]


def on_device(
    gradient, width_factor, diag_blocks, jacobi_inverse, coupling_tiles, tile_local, tile_remote, tile_count,
):
    nx, rows = lax.axis_size("cols"), lax.axis_size("rows")
    side = math.isqrt(rows // 2)
    ring = 2 * side
    width = gradient.shape[0]
    slots = tile_local.shape[0]
    blocks = BLOCKS_DEV
    half = width // 2
    vmem = pl.BlockSpec(memory_space=pltpu.VMEM)
    smem = pl.BlockSpec(memory_space=pltpu.SMEM)
    state = pltpu.VMEM((blocks, width, BLOCK), f32)
    tile_set = pltpu.VMEM((blocks, BLOCK, BLOCK), bf16)
    sem = pltpu.SemaphoreType.DMA
    scratch = [
        *[state] * 9,
        *[tile_set] * 4,
        pltpu.VMEM((2 * width, nx * width), bf16),
        pltpu.VMEM((width, nx * width), bf16),
        pltpu.VMEM((8, 128), f32),
        pltpu.VMEM((1, 128), jnp.int32),
        pltpu.VMEM((2, side, 1, 128), jnp.int32),
        pltpu.SMEM((2, side, 1, 128), jnp.int32),
        pltpu.SMEM((slots,), jnp.int32),
        pltpu.SMEM((slots,), jnp.int32),
        pltpu.SMEM((slots * blocks,), f32),
        pltpu.VMEM((2, blocks, half, BLOCK), bf16),
        *[pltpu.VMEM((side, blocks, half, BLOCK), bf16)] * 4,
        pltpu.VMEM((2, ring, side, half, BLOCK), bf16),
        *[pltpu.VMEM((ring * side, half, BLOCK), bf16)] * 4,
        state,
        pltpu.VMEM((2, nx, blocks, width, BLOCK), f32),
        pltpu.VMEM((blocks, width, BLOCK), bf16),
        pltpu.VMEM((2, nx, blocks, width, BLOCK), bf16),
        pltpu.VMEM((8, 128), f32),
        pltpu.VMEM((2, ring, 8, 128), f32),
        pltpu.VMEM((8, 128), f32),
        pltpu.VMEM((2, side, 8, 128), f32),
        pltpu.VMEM((8, 128), f32),
        pltpu.VMEM((2, nx, 8, 128), f32),
        sem((2,)), sem((2,)), sem,
        sem((2,)), sem((2, 2)),
        sem((2,)), sem((2, 2)),
        sem, sem((2,)),
        sem, sem((2,)),
        sem((3,)), sem((3, 2)),
    ]
    return pl.pallas_call(
        functools.partial(kernel, nx, side, slots, width),
        out_shape=(jax.ShapeDtypeStruct(gradient.shape, f32),) * 2,
        in_specs=[smem, smem, smem] + [vmem] * 5,
        out_specs=(vmem, vmem),
        scratch_shapes=scratch,
        compiler_params=pltpu.CompilerParams(
            collective_id=0, has_side_effects=True, vmem_limit_bytes=40 * 2**20
        ),
    )(
        tile_local, tile_remote, tile_count,
        gradient, width_factor.T, diag_blocks, jacobi_inverse, coupling_tiles,
    )


def solution(mesh):
    placed = (
        P("cols", "rows"),
        P(None, "cols"),
        P("rows", None, None),
        P("rows", None, None),
        P("rows", None, None),
        P("rows"),
        P("rows"),
        P("rows"),
    )
    return jax.shard_map(
        on_device,
        mesh=mesh,
        in_specs=placed,
        out_specs=(P("cols", "rows"), P("cols", "rows")),
        check_vma=False,
    )
```

time: 724 us -> 241 us (0.33); the launches traced: 714 us -> 241 us
  blocking collectives: 535 us -> 0 us
  Pallas kernels: 0 us -> 232 us
  waiting for transfers between devices: 47 us -> 0 us
  matrix products: 37 us -> 0 us
  starting transfers between devices: 28.4 us -> 0 us
  other arithmetic: 26.8 us -> 0 us
  local copies, waits for them, and re-layouts: 25.3 us -> 7.91 us
  between operations: 14.6 us -> 1.3 us
    psum x24 -> x0, blocking collectives: 286 us -> none  [over_axes(): return functools.reduce(lax.psum, axes, array)]
    all_to_all x10 -> x0, blocking collectives: 249 us -> none  [the longest x5 195 us: on_device(): lax.all_to_all(rounded[:, granted, :], ROWS, split_axis=1, concat_axis=1,...]
    pallas_call x0 -> x1, Pallas kernels: none -> 232 us  [on_device(): pl.pallas_call(functools.partial(kernel, nx, side, slots, width), out_sha...]
    all_to_all x3 -> x0, waiting for transfers between devices: 47 us -> none  [the longest x1 30.5 us: on_device(): lax.all_to_all(rounded[:, granted, :], ROWS, split_axis=1, concat_axis=1,...]
    dot_general x30 -> x0, matrix products: 37 us -> none  [the longest x6 13.6 us: precondition(): jnp.einsum('enj,nji->eni', blocks, jacobi_inverse, precision=highest)]
    all_to_all x3 -> x0, starting transfers between devices: 28.4 us -> none  [the longest x1 18.4 us: on_device(): lax.all_to_all(request, ROWS, split_axis=0, concat_axis=0, tiled=True)]
    gather x12 -> x0, local copies, waits for them, and re-layouts: 24.4 us -> none  [the longest x6 14.1 us: on_device(): sources = incoming[:, owner_dev, :]]
    reduce_sum x10 -> x0, other arithmetic: 12.1 us -> none  [the longest x6 7.39 us: sum_at_owner(): return arrived.sum(axis=0)]
  transfers between devices with their start and end apart: 3 -> 0, of which waited for: 3 -> 0; matrix products, arithmetic and copies ran while one was open for 0% -> 0% of each run, Pallas kernels for 0% -> 0%
where the time goes in v1:
time: 241 us
  Pallas kernels  232 us (96%)
  local copies, waits for them, and re-layouts  7.91 us (3%)
    pallas_call x1, Pallas kernels, on_device(): pl.pallas_call(functools.partial(kernel, nx, side, slots, width), out_sha...  232 us
    unnamed x16, local copies, waits for them, and re-layouts  7.91 us

profile of v1, /device:TPU:1, one launch (start us, length us, event | category | flops | bytes accessed | tf_op | source)
XLA Modules:
  0.0 240.8 jit_solution(14109402211313960447)
XLA Ops:
  1.3 0.0 copy-start
  1.3 1.6 copy-done
  2.9 0.0 copy-start.1
  2.9 1.0 copy-done.1
  3.9 0.0 copy-start.2
  3.9 1.0 copy-done.2
  5.0 0.0 copy-start.3
  5.0 0.9 copy-done.3
  5.9 0.0 copy-start.4
  5.9 0.7 copy-done.4
  6.6 0.0 copy-start.5
  6.6 0.7 copy-done.5
  7.2 0.0 copy-start.6
  7.2 0.7 copy-done.6
  7.9 231.5 %shard_map.95 = (f32[32,1024]{1,0:T(8,128)S(1)}, f32[32,1024]{1,0:T(8,128)S(1)}) custom-call(s32[64]{0:T(128)S(1)} %copy-done.5, s32[64]{0:T(128)S(1)} %copy-done.6, s32[1]{0:T(128)S(6)} %copy.12.count_s, f32[32,1024]{1,0:T(8,128)S(1)} %copy-done.3, f32[32,128]{1,0:T(8,128)S(1)} %bitcast.1, f32[8,128,128]{2,1,0:T(8,128)S(1)} %copy-done.1, ...), custom_call_target="tpu_custom_call" | custom-call | tf_op jit(solution)/shard_map/pallas_call | solution.py:386
  239.4 0.7 copy.13
  240.1 0.7 copy.14
Async XLA Ops:
  1.3 1.6 copy-start
  2.9 1.0 copy-start.1
  3.9 1.0 copy-start.2
  5.0 0.9 copy-start.3
  5.9 0.7 copy-start.4
  6.6 0.7 copy-start.5
  7.2 0.7 copy-start.6

commit v2 on v1

--- a/solution.py
+++ b/solution.py
@@ -33,18 +33,23 @@
 
 def kernel(
     nx, side, slots, width,
-    local_s, remote_s, count_s, grad_ref, wt_ref, diag_ref, jac_ref, tiles_ref,
+    local_s, remote_s, count_s, grad_hbm, wt_ref, diag_hbm, jac_hbm, tiles_hbm,
     sol_ref, res_ref,
     r, z, d, q, gz, xs, err, t, terr,
+    grad_ref, diag_ref, jac_ref, tiles_ref,
     jh, jl, dh, dl, wstack, wh, scal,
     grant_row, grant_got, grant_s, index0_s, index1_s, place_s,
-    ag_snd, ag_even_y, ag_even_z, ag_odd_y, ag_odd_z,
+    ag_snd, near_even_y, near_even_z, near_odd_y, near_odd_z,
+    far_even_y, far_even_z, far_odd_y, far_odd_z,
     aa_snd, aa_even_y, aa_even_z, aa_odd_y, aa_odd_z, xd_snd, xd_got, xc_snd, xc_got,
     ra_snd, ra_got, rb_snd, rb_got, rc_snd, rc_got,
-    g_ssem, g_rsem, g_csem, ag_ssem, ag_rsem, aa_ssem, aa_rsem, xd_ssem, xd_rsem,
+    in_sem, g_ssem, g_rsem, g_csem, ag_ssem, ag_rsem, aa_ssem, aa_rsem, xd_ssem, xd_rsem,
     xc_ssem, xc_rsem, r_ssem, r_rsem,
 ):
-    ag_got = ((ag_even_y, ag_even_z), (ag_odd_y, ag_odd_z))
+    ag_got = (
+        ((near_even_y, far_even_y), (near_even_z, far_even_z)),
+        ((near_odd_y, far_odd_y), (near_odd_z, far_odd_z)),
+    )
     aa_got = ((aa_even_y, aa_even_z), (aa_odd_y, aa_odd_z))
     blocks = BLOCKS_DEV
     half = width // 2
@@ -54,6 +59,19 @@
     y, zc = me // ring, me % ring
     zz, c = zc // 2, me % 2
     yc = y * 2 + c
+    reach = side // 4
+    far_first = sorted(range(1, side), key=lambda j: -min(j, side - j))
+    groups = (2 * reach + 1, side - 2 * reach - 1)
+    starts = (0, 2 * reach + 1)
+
+    inputs = [
+        pltpu.make_async_copy(src, dst, in_sem.at[i])
+        for i, (src, dst) in enumerate(
+            ((jac_hbm, jac_ref), (diag_hbm, diag_ref), (grad_hbm, grad_ref), (tiles_hbm, tiles_ref))
+        )
+    ]
+    for copy in inputs:
+        copy.start()
 
     def along_y(i):
         return i * ring + zc
@@ -114,12 +132,14 @@
         owner = remote_s[k] // blocks
         row = jnp.where(lanes == jnp.where(live, owner, -1), local, row)
         oy, ozc = owner // ring, owner % ring
-        index0_s[k] = ozc * side + oy
-        index1_s[k] = (oy * 2 + owner % 2) * side + ozc // 2
+        index0_s[k] = ozc * side + (oy - y + side + reach) % side
+        index1_s[k] = (oy * 2 + owner % 2) * side + (ozc // 2 - zz + side + reach) % side
         placed = jnp.where(live, local, blocks)
         for n in range(blocks):
             place_s[k * blocks + n] = jnp.where(placed == n, 1.0, 0.0).astype(f32)
     grant_row[...] = row
+    for copy in inputs[:3]:
+        copy.wait()
 
     for n in range(blocks):
         high, low = split(jac_ref[n])
@@ -200,6 +220,11 @@
         rows.append(jnp.zeros((8 - len(rows), 128), f32))
         return jnp.concatenate(rows, axis=0)
 
+    def await_ag(par, o, group, got):
+        copies = groups[group] - (1 if group == 0 else 0)
+        if copies:
+            await_got(got.at[pl.ds(0, copies)], ag_rsem.at[o, group, par])
+
     def step(e, par):
         first = e == 0
         scales = scal[...]
@@ -212,15 +237,19 @@
             terr[n] = msg.astype(f32) - tn
             ag_snd[0, n] = msg[:half]
             ag_snd[1, n] = msg[half:]
-            ag_got[par][0][y, n] = msg[:half]
-            ag_got[par][1][zz, n] = msg[half:]
-        for j in range(1, side):
-            push(ag_snd.at[0], ag_got[par][0].at[y], ag_ssem.at[0], ag_rsem.at[0, par],
-                 {"rows": along_y((y + j) % side)})
-            push(ag_snd.at[1], ag_got[par][1].at[zz], ag_ssem.at[1], ag_rsem.at[1, par],
-                 {"rows": along_z((zz + j) % side)})
-
+            ag_got[par][0][0][reach, n] = msg[:half]
+            ag_got[par][1][0][reach, n] = msg[half:]
         sums(par, inner([(d, q), (q, z), (q, t)]))
+        for group in range(2):
+            for off in far_first:
+                slot = (off + reach) % side - starts[group]
+                if 0 <= slot < groups[group]:
+                    push(ag_snd.at[0], ag_got[par][0][group].at[slot],
+                         ag_ssem.at[0, group], ag_rsem.at[0, group, par],
+                         {"rows": along_y((y - off + side) % side)})
+                    push(ag_snd.at[1], ag_got[par][1][group].at[slot],
+                         ag_ssem.at[1, group], ag_rsem.at[1, group, par],
+                         {"rows": along_z((zz - off + side) % side)})
 
         for n in range(blocks):
             part = times_tile(t[n], dh, dl, n)
@@ -231,20 +260,37 @@
 
         sums_y(par)
 
-        for o in range(2):
-            await_got(ag_got[par][o].at[pl.ds(0, side - 1)], ag_rsem.at[o, par])
-            for i in range(ring):
-                column = in_zc(i) if o == 0 else in_yc(i)
-                for s in range(side):
-                    aa_snd[o, i, s] = ag_got[par][o][s, grant_s[o, s, 0, column]]
-            mine = zc if o == 0 else yc
-            for j in range(1, ring):
-                i = (mine + j) % ring
-                push(aa_snd.at[o, i], aa_got[par][o].at[pl.ds(mine * side, side)],
-                     aa_ssem.at[o], aa_rsem.at[o, par],
-                     {"rows": in_zc(i) if o == 0 else in_yc(i)})
-            for s in range(side):
-                aa_got[par][o][mine * side + s] = aa_snd[o, mine, s]
+        if par == 0:
+            @pl.when(first)
+            def _():
+                for o in range(2):
+                    await_got(grant_got.at[o, pl.ds(0, side - 1)], g_rsem.at[o])
+                    await_sent(grant_got.at[o, pl.ds(0, side - 1)], g_ssem.at[o])
+                tables = pltpu.make_async_copy(grant_got, grant_s, g_csem)
+                tables.start()
+                tables.wait()
+
+        for group in range(2):
+            size, start = groups[group], starts[group]
+            for o in range(2):
+                got = ag_got[par][o][group]
+                await_ag(par, o, group, got)
+                at = y if o == 0 else zz
+                for i in range(ring):
+                    column = in_zc(i) if o == 0 else in_yc(i)
+                    for s in range(size):
+                        source = (at + start + s - reach + side) % side
+                        aa_snd[o, i, start + s] = got[s, grant_s[o, source, 0, column]]
+                mine = zc if o == 0 else yc
+                middle = zz if o == 0 else y
+                to = [((middle + off) % side) * 2 + k for off in far_first for k in range(2)]
+                for i in [*to, middle * 2 + 1 - c]:
+                    push(aa_snd.at[o, i, pl.ds(start, size)],
+                         aa_got[par][o].at[pl.ds(mine * side + start, size)],
+                         aa_ssem.at[o, group], aa_rsem.at[o, group, par],
+                         {"rows": in_zc(i) if o == 0 else in_yc(i)})
+                for s in range(start, start + size):
+                    aa_got[par][o][mine * side + s] = aa_snd[o, mine, s]
 
         sums_x(par)
         total = sums_end(par)
@@ -265,10 +311,16 @@
             d[n] = zn + b * dn
             err[n] = err[n] - a * terr[n]
 
+        if par == 0:
+            @pl.when(first)
+            def _():
+                inputs[3].wait()
         for o in range(2):
-            await_got(aa_got[par][o].at[pl.ds(0, (ring - 1) * side)], aa_rsem.at[o, par])
-
-        unroll = 16
+            for group in range(2):
+                amount = (ring - 1) * groups[group]
+                await_got(aa_got[par][o].at[pl.ds(0, amount)], aa_rsem.at[o, group, par])
+
+        unroll = min(32, slots)
 
         def tiles(group, sums_of):
             sums_of = list(sums_of)
@@ -288,7 +340,7 @@
             part = coupled[n].astype(bf16)
             xc_snd[n] = part
             xc_got[par, mx, n] = part
-        for j in range(1, nx):
+        for j in sorted(range(1, nx), key=lambda j: -min(j, nx - j)):
             push(xc_snd, xc_got.at[par, mx], xc_ssem, xc_rsem.at[par], {"cols": (mx + j) % nx})
         await_got(xd_got.at[par, pl.ds(0, nx - 1)], xd_rsem.at[par])
         await_got(xc_got.at[par, pl.ds(0, nx - 1)], xc_rsem.at[par])
@@ -305,17 +357,14 @@
             q[n] = gn + b * q[n]
 
         for o in range(2):
-            await_sent(ag_got[par][o].at[pl.ds(0, side - 1)], ag_ssem.at[o])
-            await_sent(aa_got[par][o].at[pl.ds(0, (ring - 1) * side)], aa_ssem.at[o])
+            for group in range(2):
+                copies = groups[group] - (1 if group == 0 else 0)
+                if copies:
+                    await_sent(ag_got[par][o][group].at[pl.ds(0, copies)], ag_ssem.at[o, group])
+                amount = (ring - 1) * groups[group]
+                await_sent(aa_got[par][o].at[pl.ds(0, amount)], aa_ssem.at[o, group])
         await_sent(xd_got.at[par, pl.ds(0, nx - 1)], xd_ssem)
         await_sent(xc_got.at[par, pl.ds(0, nx - 1)], xc_ssem)
-
-    for o in range(2):
-        await_got(grant_got.at[o, pl.ds(0, side - 1)], g_rsem.at[o])
-        await_sent(grant_got.at[o, pl.ds(0, side - 1)], g_ssem.at[o])
-    tables = pltpu.make_async_copy(grant_got, grant_s, g_csem)
-    tables.start()
-    tables.wait()
 
     def two_steps(i, carry):
         step(2 * i, 0)
@@ -345,13 +394,19 @@
     slots = tile_local.shape[0]
     blocks = BLOCKS_DEV
     half = width // 2
+    near = 2 * (side // 4) + 1
     vmem = pl.BlockSpec(memory_space=pltpu.VMEM)
     smem = pl.BlockSpec(memory_space=pltpu.SMEM)
+    hbm = pl.BlockSpec(memory_space=pltpu.HBM)
     state = pltpu.VMEM((blocks, width, BLOCK), f32)
     tile_set = pltpu.VMEM((blocks, BLOCK, BLOCK), bf16)
     sem = pltpu.SemaphoreType.DMA
     scratch = [
         *[state] * 9,
+        pltpu.VMEM(gradient.shape, f32),
+        pltpu.VMEM((blocks, BLOCK, BLOCK), f32),
+        pltpu.VMEM((blocks, BLOCK, BLOCK), f32),
+        pltpu.VMEM((slots, BLOCK, BLOCK), bf16),
         *[tile_set] * 4,
         pltpu.VMEM((2 * width, nx * width), bf16),
         pltpu.VMEM((width, nx * width), bf16),
@@ -363,7 +418,8 @@
         pltpu.SMEM((slots,), jnp.int32),
         pltpu.SMEM((slots * blocks,), f32),
         pltpu.VMEM((2, blocks, half, BLOCK), bf16),
-        *[pltpu.VMEM((side, blocks, half, BLOCK), bf16)] * 4,
+        *[pltpu.VMEM((near, blocks, half, BLOCK), bf16)] * 4,
+        *[pltpu.VMEM((side - near, blocks, half, BLOCK), bf16)] * 4,
         pltpu.VMEM((2, ring, side, half, BLOCK), bf16),
         *[pltpu.VMEM((ring * side, half, BLOCK), bf16)] * 4,
         state,
@@ -376,9 +432,9 @@
         pltpu.VMEM((2, side, 8, 128), f32),
         pltpu.VMEM((8, 128), f32),
         pltpu.VMEM((2, nx, 8, 128), f32),
-        sem((2,)), sem((2,)), sem,
-        sem((2,)), sem((2, 2)),
-        sem((2,)), sem((2, 2)),
+        sem((4,)), sem((2,)), sem((2,)), sem,
+        sem((2, 2)), sem((2, 2, 2)),
+        sem((2, 2)), sem((2, 2, 2)),
         sem, sem((2,)),
         sem, sem((2,)),
         sem((3,)), sem((3, 2)),
@@ -386,7 +442,7 @@
     return pl.pallas_call(
         functools.partial(kernel, nx, side, slots, width),
         out_shape=(jax.ShapeDtypeStruct(gradient.shape, f32),) * 2,
-        in_specs=[smem, smem, smem] + [vmem] * 5,
+        in_specs=[smem, smem, smem, hbm, vmem, hbm, hbm, hbm],
         out_specs=(vmem, vmem),
         scratch_shapes=scratch,
         compiler_params=pltpu.CompilerParams(

time: 241 us -> 202 us (0.84)
  Pallas kernels: 232 us -> 192 us
    pallas_call x1, Pallas kernels: 232 us -> 192 us  [on_device(): pl.pallas_call(functools.partial(kernel, nx, side, slots, width), out_sha...]
where the time goes in v2:
time: 202 us; the launch traced here: 201 us
  Pallas kernels  192 us (95%)
  local copies, waits for them, and re-layouts  7.91 us (4%)
    pallas_call x1, Pallas kernels, on_device(): pl.pallas_call(functools.partial(kernel, nx, side, slots, width), out_sha...  192 us
    unnamed x16, local copies, waits for them, and re-layouts  7.91 us

profile of v2, /device:TPU:1, one launch (start us, length us, event | category | flops | bytes accessed | tf_op | source)
XLA Modules:
  0.0 201.3 jit_solution(15627384432613010121)
XLA Ops:
  1.3 0.0 copy-start
  1.3 1.6 copy-done
  2.9 0.0 copy-start.1
  2.9 1.0 copy-done.1
  3.9 0.0 copy-start.2
  3.9 1.0 copy-done.2
  5.0 0.0 copy-start.3
  5.0 0.9 copy-done.3
  5.9 0.0 copy-start.4
  5.9 0.7 copy-done.4
  6.6 0.0 copy-start.5
  6.6 0.7 copy-done.5
  7.2 0.0 copy-start.6
  7.2 0.7 copy-done.6
  7.9 192.1 %shard_map.95 = (f32[32,1024]{1,0:T(8,128)S(1)}, f32[32,1024]{1,0:T(8,128)S(1)}) custom-call(s32[64]{0:T(128)S(1)} %copy-done.5, s32[64]{0:T(128)S(1)} %copy-done.6, s32[1]{0:T(128)S(6)} %copy.12.count_s, f32[32,1024]{1,0:T(8,128)S(1)} %copy-done.3, f32[32,128]{1,0:T(8,128)S(1)} %bitcast.1, f32[8,128,128]{2,1,0:T(8,128)S(1)} %copy-done.1, ...), custom_call_target="tpu_custom_call" | custom-call | tf_op jit(solution)/shard_map/pallas_call | solution.py:442
  200.0 0.7 copy.13
  200.6 0.7 copy.14
Async XLA Ops:
  1.3 1.6 copy-start
  2.9 1.0 copy-start.1
  3.9 1.0 copy-start.2
  5.0 0.9 copy-start.3
  5.9 0.7 copy-start.4
  6.6 0.7 copy-start.5
  7.2 0.7 copy-start.6

commit v3 on v2

--- a/solution.py
+++ b/solution.py
@@ -446,7 +446,7 @@
         out_specs=(vmem, vmem),
         scratch_shapes=scratch,
         compiler_params=pltpu.CompilerParams(
-            collective_id=0, has_side_effects=True, vmem_limit_bytes=40 * 2**20
+            collective_id=0, has_side_effects=True, vmem_limit_bytes=67_043_328
         ),
     )(
         tile_local, tile_remote, tile_count,

time: 202 us -> 198 us (0.980)
  local copies, waits for them, and re-layouts: 7.91 us -> 3.14 us
    unnamed x16 -> x2, local copies, waits for them, and re-layouts: 7.91 us -> 3.14 us
where the time goes in v3:
time: 198 us; the launch traced here: 197 us
  Pallas kernels  193 us (97%)
  local copies, waits for them, and re-layouts  3.14 us (2%)
    pallas_call x1, Pallas kernels, on_device(): pl.pallas_call(functools.partial(kernel, nx, side, slots, width), out_sha...  193 us

profile of v3, /device:TPU:1, one launch (start us, length us, event | category | flops | bytes accessed | tf_op | source)
XLA Modules:
  0.0 197.1 jit_solution(13919969400621655856)
XLA Ops:
  1.3 192.7 %shard_map.95 = (f32[32,1024]{1,0:T(8,128)}, f32[32,1024]{1,0:T(8,128)}) custom-call(s32[64]{0:T(128)} %local_s.1, s32[64]{0:T(128)} %remote_s.1, s32[1]{0:T(128)S(6)} %copy.12.count_s, f32[32,1024]{1,0:T(8,128)} %grad_hbm.1, f32[32,128]{1,0:T(8,128)} %bitcast.1, f32[8,128,128]{2,1,0:T(8,128)} %diag_hbm.1, f32[8,128,128]{2,1,0:T(8,128)} %jac_hbm.1, ...), custom_call_target="tpu_custom_call" | custom-call | tf_op jit(solution)/shard_map/pallas_call | solution.py:442
  194.0 1.6 copy.13
  195.6 1.6 copy.14
